TPU v7x, 32 devices: a whole 2x2x4 slice. The times are simulated.
32 devices in a mesh: blk: 16 (over z, y, core), grp: 2 (over x).
Axes of the slice: x: 2, y: 2, z: 4, core: 2. Of those that a mesh axis runs over, the one named last changes fastest.
Arguments:
- layer_one: bfloat16 [1792, 1024], P(('blk', 'grp')), may hold values from -6 to 6
- layer_two: bfloat16 [1792, 1024], P(('blk', 'grp')), may hold values from -6 to 6
- spread: int32 [2], replicated, may hold values from 1024 to 4096
Outputs:
- profiles: float32 [2, 1792], P(None, ('blk', 'grp'))
- alignment: float32 [], replicated
All inputs are finite; a program needn't handle non-finite values.
Results may differ from a plain program's by a relative error of at most 0.0003.
Values may be sent and summed in bfloat16 or wider, within the bound.
A program may use at most 128 MiB of HBM per device.

v0:
```python
import jax
import jax.numpy as jnp
from jax import lax
from jax.sharding import PartitionSpec as P

D = 1024


def kernel_block(rows, sq_rows, cols, scale, offset):
    sq_cols = jnp.sum(cols.astype(jnp.float32) ** 2, axis=1)
    inner = lax.dot_general(
        rows, cols, (((1,), (1,)), ((), ())), preferred_element_type=jnp.float32
    )
    dist = sq_rows[:, None] + sq_cols[None, :] - 2.0 * inner
    return jnp.exp(-dist / (2.0 * scale)) - offset


def shards(layer_one, layer_two, spread):
    scales = spread.astype(jnp.float32)
    offsets = jnp.exp(-D / scales)
    stacked = jnp.stack([layer_one, layer_two])
    paired = lax.all_gather(stacked, "grp", axis=1, tiled=True)
    sq_pair = jnp.sum(paired.astype(jnp.float32) ** 2, axis=2)
    block = lax.all_gather(stacked, "blk", axis=1, tiled=True)
    first = kernel_block(paired[0], sq_pair[0], block[0], scales[0], offsets[0])
    second = kernel_block(paired[1], sq_pair[1], block[1], scales[1], offsets[1])
    first, second = (first, second)
    rows_acc = jnp.stack([jnp.sum(first, axis=1), jnp.sum(second, axis=1)])
    prods = jnp.stack([jnp.sum(first * second), jnp.sum(first * first), jnp.sum(second * second)])
    rows_acc, prods = (rows_acc, prods)
    own_rows = lax.psum_scatter(rows_acc, "grp", scatter_dimension=1, tiled=True)
    total = own_rows.shape[1] * lax.axis_size("blk") * lax.axis_size("grp")
    row_terms = jnp.stack(
        [
            jnp.sum(own_rows[0]),
            jnp.sum(own_rows[1]),
            jnp.sum(own_rows[0] * own_rows[1]),
            jnp.sum(own_rows[0] * own_rows[0]),
            jnp.sum(own_rows[1] * own_rows[1]),
        ]
    )
    prods = lax.psum(prods, ("blk", "grp"))
    row_terms = lax.psum(row_terms, ("blk", "grp"))
    sum_one, sum_two = (row_terms[0], row_terms[1])
    c_cross, c_one, c_two = (row_terms[2], row_terms[3], row_terms[4])
    h_cross = prods[0] - 2.0 * c_cross / total + sum_one * sum_two / (total * total)
    h_one = prods[1] - 2.0 * c_one / total + sum_one * sum_one / (total * total)
    h_two = prods[2] - 2.0 * c_two / total + sum_two * sum_two / (total * total)
    alignment = h_cross / jnp.sqrt(h_one * h_two)
    profiles = jnp.stack(
        [own_rows[0] / jnp.sqrt(c_one / total), own_rows[1] / jnp.sqrt(c_two / total)]
    )
    return (profiles, alignment)


def solution(mesh):
    return jax.shard_map(
        shards,
        mesh=mesh,
        in_specs=(P(("blk", "grp"), None), P(("blk", "grp"), None), P()),
        out_specs=(P(None, ("blk", "grp")), P()),
        check_vma=False,
    )
```

profile of v0, /device:TPU:0, one launch (start us, length us, event | category | flops | bytes accessed | tf_op | source)
XLA Modules:
  0.0 135.6 jit_solution(13423032327136159622)
XLA Ops:
  7.2 0.0 all-gather.2.cloned.1.call-start
  7.2 1.7 %pad_maximum_fusion = bf16[2,56,1024]{2,1,0:T(8,128)(2,1)} fusion(bf16[1,56,1024]{2,1,0:T(8,128)(2,1)} %bitcast.70, bf16[1,56,1024]{2,1,0:T(8,128)(2,1)} %bitcast.71), kind=kLoop, calls=%fused_computation.24 | loop fusion | flops 114688 | bytes 458752 | tf_op jit(solution)/shard_map/stack | solution.py:21
  8.9 0.0 all-gather.2.cloned.1.call-update
  8.9 0.7 convert_element_type.14
  9.6 0.6 fusion.16
  11.5 1.2 dynamic-slice
  13.4 0.7 divide_exponential_fusion
  14.0 0.6 fusion.17
  14.6 9.5 %all_gather.6 = bf16[2,112,1024]{2,1,0:T(8,128)(2,1)S(1)} all-gather(bf16[2,56,1024]{2,1,0:T(8,128)(2,1)} %pad_maximum_fusion), channel_id=1, replica_groups=mesh['blk'=16,'grp'=2] {'grp'}, dimensions={1}, use_global_device_ids=true | all-gather | bytes 688128 | tf_op jit(solution)/shard_map/all_gather | solution.py:22
  24.1 0.2 multiply_reduce_fusion.2
  24.3 36.4 %all-gather.2.cloned.1.call-done = bf16[2,896,1024]{2,1,0:T(8,128)(2,1)} async-done(((bf16[2,56,1024]{2,1,0:T(8,128)(2,1)}), bf16[2,896,1024]{2,1,0:T(8,128)(2,1)}) %all-gather.2.cloned.1.call-update) | async-done | bytes 3670032 | tf_op jit(solution)/shard_map/all_gather | solution.py:24
  60.7 0.0 copy-start
  60.7 3.0 %multiply_reduce_fusion.1 = (f32[896]{0:T(1024)S(1)}, f32[896]{0:T(1024)S(1)}) fusion(bf16[2,896,1024]{2,1,0:T(8,128)(2,1)} %all-gather.2.cloned.1.call-done), kind=kLoop, calls=%fused_computation.1 | loop fusion | flops 5503232 | bytes 3677184 | tf_op jit(solution)/shard_map/reduce_sum | solution.py:10
  63.7 0.2 copy-done
  63.8 1.4 %fusion.10 = f32[112,896]{1,0:T(8,128)S(1)} fusion(bf16[2,896,1024]{2,1,0:T(8,128)(2,1)S(1)} %copy-done, bf16[2,112,1024]{2,1,0:T(8,128)(2,1)S(1)} %all_gather.6, f32[]{:T(128)} %bitcast.12, f32[]{:T(128)} %bitcast.11, f32[896]{0:T(1024)S(1)} %get-tuple-element.3, f32[112]{0:T(128)S(1)} %get-tuple-element.18), kind=kOutput, calls=%fused_computation.14 | convolution fusion | flops 206123008 | bytes 2470408 | tf_op jit(solution)/shard_map/dot_general | solution.py:11
  65.2 2.1 %multiply_reduce_fusion.5 = (f32[]{:T(128)}, f32[]{:T(128)}, f32[112]{0:T(128)S(1)}, f32[]{:T(128)}, f32[112]{0:T(128)S(1)}) fusion(f32[112,896]{1,0:T(8,128)S(1)} %fusion.10, f32[]{:T(128)} %bitcast.6, f32[]{:T(128)} %bitcast.5, bf16[2,896,1024]{2,1,0:T(8,128)(2,1)S(1)} %copy-done, bf16[2,112,1024]{2,1,0:T(8,128)(2,1)S(1)} %all_gather.6, ...), kind=kOutput, calls=%fused_computation.21 | convolution fusion | flops 206925600 | bytes 2471316 | tf_op jit(solution)/shard_map/dot_general | solution.py:11
  67.4 4.9 %all-reduce = f32[2,112]{1,0:T(2,128)S(1)} all-reduce(f32[2,112]{1,0:T(2,128)S(1)} %pad_maximum_fusion.1), channel_id=2, replica_groups=mesh['blk'=16,'grp'=2] {'grp'}, use_global_device_ids=true, to_apply=%region_5.0.clone | all-reduce | flops 224 | bytes 1792
  72.3 0.1 constant_dynamic-slice_fusion
  72.4 0.7 multiply_reduce_fusion.6
  73.0 2.0 %pad_maximum_fusion.3 = f32[3]{0:T(128)S(1)} fusion(f32[1]{0:T(128)} %bitcast.23, f32[1]{0:T(128)} %bitcast.22, f32[1]{0:T(128)} %bitcast.21), kind=kLoop, calls=%fused_computation.27 | loop fusion | flops 6 | bytes 24 | tf_op jit(solution)/shard_map/stack | solution.py:29
  75.0 3.2 %stack.64 = f32[5]{0:T(128)S(1)} concatenate(f32[1]{0:T(128)} %bitcast.14, f32[1]{0:T(128)} %bitcast.15, f32[1]{0:T(128)} %bitcast.16, f32[1]{0:T(128)} %bitcast.17, f32[1]{0:T(128)} %bitcast.18), dimensions={0} | concatenate | bytes 40 | tf_op jit(solution)/shard_map/stack | solution.py:33
  78.2 39.4 %all-reduce.1 = (f32[5]{0:T(128)S(1)}, f32[3]{0:T(128)S(1)}) all-reduce(f32[5]{0:T(128)S(1)} %stack.64, f32[3]{0:T(128)S(1)} %pad_maximum_fusion.3), channel_id=1, replica_groups=mesh['blk'=16,'grp'=2] {'blk','grp'}, use_global_device_ids=true, to_apply=%region_11.0 | all-reduce | flops 8 | bytes 64 | tf_op jit(solution)/shard_map/psum | solution.py:43
  117.6 0.7 fusion.14
  127.1 0.6 pad_maximum_fusion.2
  (3 shorter events, 0.0 us)
Async XLA Ops:
  7.2 53.5 %all-gather.2.cloned.1.call-start = ((), (), s32[]{:S(2)}) async-start(), calls=%async_computation | async-start | bytes 3899392 | tf_op jit(solution)/shard_map/all_gather | solution.py:24
  60.7 3.1 %copy-start = (bf16[2,896,1024]{2,1,0:T(8,128)(2,1)S(1)}, bf16[2,896,1024]{2,1,0:T(8,128)(2,1)}, u32[]{:S(2)}) copy-start(bf16[2,896,1024]{2,1,0:T(8,128)(2,1)} %all-gather.2.cloned.1.call-done) | copy-start | bytes 11010052
Sparse Core Ops, SparseCore 0:
  10.3 50.3 all-gather.1
where the time goes:
time: 136 us
  blocking collectives  53.8 us (40%)
  waiting for transfers between devices  36.4 us (27%)
  between operations  26 us (19%)
  other arithmetic  9.38 us (7%)
  local copies, waits for them, and re-layouts  6.55 us (5%)
  matrix products  3.5 us (3%)
    psum x1, blocking collectives, shards(): row_terms = lax.psum(row_terms, ('blk', 'grp'))  39.4 us
    all_gather x1, waiting for transfers between devices, shards(): block = lax.all_gather(stacked, 'blk', axis=1, tiled=True)  36.4 us
    all_gather x1, blocking collectives, shards(): paired = lax.all_gather(stacked, 'grp', axis=1, tiled=True)  9.49 us
    unnamed x1, blocking collectives  4.91 us
    dot_general x2, matrix products, kernel_block(): lax.dot_general(rows, cols, (((1,), (1,)), ((), ())), preferred_element_t...  3.5 us
    another operation x1, local copies, waits for them, and re-layouts, shards(): jnp.stack([jnp.sum(own_rows[0]), jnp.sum(own_rows[1]), jnp.sum(own_rows[0...  3.22 us
    reduce_sum x1, other arithmetic, kernel_block(): sq_cols = jnp.sum(cols.astype(jnp.float32) ** 2, axis=1)  2.99 us
  transfers between devices with their start and end apart: 1, of which 1 were waited for; matrix products, arithmetic and copies ran while one was open for 3% of the time, Pallas kernels for 0%

commit v1 on v0

--- a/solution.py
+++ b/solution.py
@@ -21,7 +21,13 @@
     stacked = jnp.stack([layer_one, layer_two])
     paired = lax.all_gather(stacked, "grp", axis=1, tiled=True)
     sq_pair = jnp.sum(paired.astype(jnp.float32) ** 2, axis=2)
-    block = lax.all_gather(stacked, "blk", axis=1, tiled=True)
+    count = lax.axis_size("blk")
+    moving, blocks = (stacked, [stacked])
+    for _ in range(count - 1):
+        moving = lax.ppermute(moving, "blk", [(i, (i + 1) % count) for i in range(count)])
+        blocks.insert(0, moving)
+    line = jnp.concatenate(blocks, axis=1)
+    block = jnp.roll(line, (lax.axis_index("blk") + 1) * stacked.shape[1], axis=1)
     first = kernel_block(paired[0], sq_pair[0], block[0], scales[0], offsets[0])
     second = kernel_block(paired[1], sq_pair[1], block[1], scales[1], offsets[1])
     first, second = (first, second)

time: 136 us -> 197 us (1.45)
  waiting for transfers between devices: 36.4 us -> 110 us
  between operations: 26 us -> 12.8 us
  local copies, waits for them, and re-layouts: 6.55 us -> 12.3 us
  blocking collectives: 53.8 us -> 48.4 us
  other arithmetic: 9.38 us -> 7.06 us
    ppermute x0 -> x15, waiting for transfers between devices: none -> 110 us  [shards(): lax.ppermute(moving, 'blk', [(i, (i + 1) % count) for i in range(count)])]
    all_gather x1 -> x0, waiting for transfers between devices: 36.4 us -> none  [shards(): block = lax.all_gather(stacked, 'blk', axis=1, tiled=True)]
    unnamed x4 -> x40, local copies, waits for them, and re-layouts: 1.47 us -> 7.25 us
    all_gather x1, blocking collectives: 9.49 us -> 6.68 us  [shards(): paired = lax.all_gather(stacked, 'grp', axis=1, tiled=True)]
    psum x1, blocking collectives: 39.4 us -> 36.8 us  [shards(): row_terms = lax.psum(row_terms, ('blk', 'grp'))]
  transfers between devices with their start and end apart: 1 -> 15, of which waited for: 1 -> 15; matrix products, arithmetic and copies ran while one was open for 3% -> 2% of each run, Pallas kernels for 0% -> 0%
where the time goes in v1:
time: 197 us; the launch traced here: 195 us
  waiting for transfers between devices  110 us (56%)
  blocking collectives  48.4 us (25%)
  between operations  12.8 us (6%)
  local copies, waits for them, and re-layouts  12.3 us (6%)
  other arithmetic  7.06 us (4%)
  matrix products  3.51 us (2%)
    ppermute x15, waiting for transfers between devices, shards(): lax.ppermute(moving, 'blk', [(i, (i + 1) % count) for i in range(count)])  110 us
    psum x1, blocking collectives, shards(): row_terms = lax.psum(row_terms, ('blk', 'grp'))  36.8 us
    unnamed x40, local copies, waits for them, and re-layouts  7.25 us
    all_gather x1, blocking collectives, shards(): paired = lax.all_gather(stacked, 'grp', axis=1, tiled=True)  6.68 us
    unnamed x1, blocking collectives  4.91 us
  transfers between devices with their start and end apart: 15, of which 15 were waited for; matrix products, arithmetic and copies ran while one was open for 2% of the time, Pallas kernels for 0%

profile of v1, /device:TPU:0, one launch (start us, length us, event | category | flops | bytes accessed | tf_op | source)
XLA Modules:
  0.0 195.2 jit_solution(2756869121061232474)
XLA Ops:
  0.6 1.0 pad_maximum_fusion
  2.2 8.7 %collective-permute-done = bf16[2,56,1024]{2,1,0:T(8,128)(2,1)S(1)} collective-permute-done((bf16[2,56,1024]{2,1,0:T(8,128)(2,1)S(1)}, bf16[2,56,1024]{2,1,0:T(8,128)(2,1)S(1)}, u32[]{:S(2)}, u32[]{:S(2)}) %collective-permute-start) | collective-permute-done | bytes 229408 | tf_op jit(solution)/shard_map/ppermute | solution.py:27
  10.9 8.1 %collective-permute-done.1 = bf16[2,56,1024]{2,1,0:T(8,128)(2,1)S(1)} collective-permute-done((bf16[2,56,1024]{2,1,0:T(8,128)(2,1)S(1)}, bf16[2,56,1024]{2,1,0:T(8,128)(2,1)S(1)}, u32[]{:S(2)}, u32[]{:S(2)}) %collective-permute-start.1) | collective-permute-done | bytes 229408 | tf_op jit(solution)/shard_map/ppermute | solution.py:27
  19.0 8.1 %collective-permute-done.2 = bf16[2,56,1024]{2,1,0:T(8,128)(2,1)S(1)} collective-permute-done((bf16[2,56,1024]{2,1,0:T(8,128)(2,1)S(1)}, bf16[2,56,1024]{2,1,0:T(8,128)(2,1)S(1)}, u32[]{:S(2)}, u32[]{:S(2)}) %collective-permute-start.2) | collective-permute-done | bytes 229408 | tf_op jit(solution)/shard_map/ppermute | solution.py:27
  27.2 8.1 %collective-permute-done.3 = bf16[2,56,1024]{2,1,0:T(8,128)(2,1)S(1)} collective-permute-done((bf16[2,56,1024]{2,1,0:T(8,128)(2,1)S(1)}, bf16[2,56,1024]{2,1,0:T(8,128)(2,1)S(1)}, u32[]{:S(2)}, u32[]{:S(2)}) %collective-permute-start.3) | collective-permute-done | bytes 229408 | tf_op jit(solution)/shard_map/ppermute | solution.py:27
  35.3 8.1 %collective-permute-done.4 = bf16[2,56,1024]{2,1,0:T(8,128)(2,1)S(1)} collective-permute-done((bf16[2,56,1024]{2,1,0:T(8,128)(2,1)S(1)}, bf16[2,56,1024]{2,1,0:T(8,128)(2,1)S(1)}, u32[]{:S(2)}, u32[]{:S(2)}) %collective-permute-start.4) | collective-permute-done | bytes 229408 | tf_op jit(solution)/shard_map/ppermute | solution.py:27
  43.5 8.1 %collective-permute-done.5 = bf16[2,56,1024]{2,1,0:T(8,128)(2,1)S(1)} collective-permute-done((bf16[2,56,1024]{2,1,0:T(8,128)(2,1)S(1)}, bf16[2,56,1024]{2,1,0:T(8,128)(2,1)S(1)}, u32[]{:S(2)}, u32[]{:S(2)}) %collective-permute-start.5) | collective-permute-done | bytes 229408 | tf_op jit(solution)/shard_map/ppermute | solution.py:27
  51.6 8.1 %collective-permute-done.6 = bf16[2,56,1024]{2,1,0:T(8,128)(2,1)S(1)} collective-permute-done((bf16[2,56,1024]{2,1,0:T(8,128)(2,1)S(1)}, bf16[2,56,1024]{2,1,0:T(8,128)(2,1)S(1)}, u32[]{:S(2)}, u32[]{:S(2)}) %collective-permute-start.6) | collective-permute-done | bytes 229408 | tf_op jit(solution)/shard_map/ppermute | solution.py:27
  59.8 8.1 %collective-permute-done.7 = bf16[2,56,1024]{2,1,0:T(8,128)(2,1)S(1)} collective-permute-done((bf16[2,56,1024]{2,1,0:T(8,128)(2,1)S(1)}, bf16[2,56,1024]{2,1,0:T(8,128)(2,1)S(1)}, u32[]{:S(2)}, u32[]{:S(2)}) %collective-permute-start.7) | collective-permute-done | bytes 229408 | tf_op jit(solution)/shard_map/ppermute | solution.py:27
  67.9 8.1 %collective-permute-done.8 = bf16[2,56,1024]{2,1,0:T(8,128)(2,1)S(1)} collective-permute-done((bf16[2,56,1024]{2,1,0:T(8,128)(2,1)S(1)}, bf16[2,56,1024]{2,1,0:T(8,128)(2,1)S(1)}, u32[]{:S(2)}, u32[]{:S(2)}) %collective-permute-start.8) | collective-permute-done | bytes 229408 | tf_op jit(solution)/shard_map/ppermute | solution.py:27
  76.1 8.1 %collective-permute-done.9 = bf16[2,56,1024]{2,1,0:T(8,128)(2,1)S(1)} collective-permute-done((bf16[2,56,1024]{2,1,0:T(8,128)(2,1)S(1)}, bf16[2,56,1024]{2,1,0:T(8,128)(2,1)S(1)}, u32[]{:S(2)}, u32[]{:S(2)}) %collective-permute-start.9) | collective-permute-done | bytes 229408 | tf_op jit(solution)/shard_map/ppermute | solution.py:27
  84.2 8.1 %collective-permute-done.10 = bf16[2,56,1024]{2,1,0:T(8,128)(2,1)S(1)} collective-permute-done((bf16[2,56,1024]{2,1,0:T(8,128)(2,1)S(1)}, bf16[2,56,1024]{2,1,0:T(8,128)(2,1)S(1)}, u32[]{:S(2)}, u32[]{:S(2)}) %collective-permute-start.10) | collective-permute-done | bytes 229408 | tf_op jit(solution)/shard_map/ppermute | solution.py:27
  93.0 7.5 %collective-permute-done.11 = bf16[2,56,1024]{2,1,0:T(8,128)(2,1)S(1)} collective-permute-done((bf16[2,56,1024]{2,1,0:T(8,128)(2,1)S(1)}, bf16[2,56,1024]{2,1,0:T(8,128)(2,1)S(1)}, u32[]{:S(2)}, u32[]{:S(2)}) %collective-permute-start.11) | collective-permute-done | bytes 229408 | tf_op jit(solution)/shard_map/ppermute | solution.py:27
  100.5 6.7 %all_gather.3 = bf16[2,112,1024]{2,1,0:T(8,128)(2,1)S(1)} all-gather(bf16[2,56,1024]{2,1,0:T(8,128)(2,1)S(1)} %pad_maximum_fusion), channel_id=1, replica_groups=mesh['blk'=16,'grp'=2] {'grp'}, dimensions={1}, use_global_device_ids=true | all-gather | bytes 688128 | tf_op jit(solution)/shard_map/all_gather | solution.py:22
  107.3 1.3 collective-permute-done.12
  110.6 7.0 %collective-permute-done.13 = bf16[2,56,1024]{2,1,0:T(8,128)(2,1)} collective-permute-done((bf16[2,56,1024]{2,1,0:T(8,128)(2,1)S(1)}, bf16[2,56,1024]{2,1,0:T(8,128)(2,1)}, u32[]{:S(2)}, u32[]{:S(2)}) %collective-permute-start.13) | collective-permute-done | bytes 229408 | tf_op jit(solution)/shard_map/ppermute | solution.py:27
  119.4 1.3 dynamic-slice
  121.3 4.7 %collective-permute-done.14 = bf16[2,56,1024]{2,1,0:T(8,128)(2,1)} collective-permute-done((bf16[2,56,1024]{2,1,0:T(8,128)(2,1)}, bf16[2,56,1024]{2,1,0:T(8,128)(2,1)}, u32[]{:S(2)}, u32[]{:S(2)}) %collective-permute-start.14) | collective-permute-done | bytes 229408 | tf_op jit(solution)/shard_map/ppermute | solution.py:27
  126.0 1.0 constant_dynamic-update-slice_fusion.31
  127.0 1.0 constant_dynamic-update-slice_fusion.30
  127.9 1.0 constant_dynamic-update-slice_fusion.29
  129.2 1.0 constant_dynamic-update-slice_fusion.15
  130.2 1.0 constant_dynamic-update-slice_fusion.14
  131.5 1.3 multiply_reduce_fusion.1
  132.8 1.4 exponential_subtract_fusion
  134.2 2.1 %multiply_reduce_fusion.5 = (f32[]{:T(128)}, f32[]{:T(128)}, f32[112]{0:T(128)S(1)}, f32[]{:T(128)}, f32[112]{0:T(128)S(1)}) fusion(f32[112,896]{1,0:T(8,128)S(1)} %exponential_subtract_fusion, f32[]{:T(128)} %bitcast.6, f32[]{:T(128)} %bitcast.5, bf16[2,1792,1024]{2,1,0:T(8,128)(2,1)S(1)} %constant_dynamic-update-slice_fusion, s32[]{:T(128)S(6)} %select_n.14, ...), kind=kOutput, calls=%fused_computation.11 | convolution fusion | flops 206925600 | bytes 2471320 | tf_op jit(solution)/shard_map/dot_general | solution.py:11
  136.3 4.9 %all-reduce = f32[2,112]{1,0:T(2,128)S(1)} all-reduce(f32[2,112]{1,0:T(2,128)S(1)} %pad_maximum_fusion.1), channel_id=2, replica_groups=mesh['blk'=16,'grp'=2] {'grp'}, use_global_device_ids=true, to_apply=%region_5.6.clone | all-reduce | flops 224 | bytes 1792
  141.3 0.7 multiply_reduce_fusion.6
  142.0 2.0 %pad_maximum_fusion.3 = f32[3]{0:T(128)S(1)} fusion(f32[1]{0:T(128)} %bitcast.23, f32[1]{0:T(128)} %bitcast.22, f32[1]{0:T(128)} %bitcast.21), kind=kLoop, calls=%fused_computation.51 | loop fusion | flops 6 | bytes 24 | tf_op jit(solution)/shard_map/stack | solution.py:35
  144.0 3.2 %stack.64 = f32[5]{0:T(128)S(1)} concatenate(f32[1]{0:T(128)} %bitcast.14, f32[1]{0:T(128)} %bitcast.15, f32[1]{0:T(128)} %bitcast.16, f32[1]{0:T(128)} %bitcast.17, f32[1]{0:T(128)} %bitcast.18), dimensions={0} | concatenate | bytes 40 | tf_op jit(solution)/shard_map/stack | solution.py:39
  147.2 36.8 %all-reduce.1 = (f32[5]{0:T(128)S(1)}, f32[3]{0:T(128)S(1)}) all-reduce(f32[5]{0:T(128)S(1)} %stack.64, f32[3]{0:T(128)S(1)} %pad_maximum_fusion.3), channel_id=1, replica_groups=mesh['blk'=16,'grp'=2] {'blk','grp'}, use_global_device_ids=true, to_apply=%region_11.12 | all-reduce | flops 8 | bytes 64 | tf_op jit(solution)/shard_map/psum | solution.py:49
  184.0 0.7 fusion.6
  (60 shorter events, 5.1 us)
Async XLA Ops:
  0.6 128.6 %copy-start.1 = (bf16[56,1024]{1,0:T(8,128)(2,1)S(1)}, bf16[56,1024]{1,0:T(8,128)(2,1)}, u32[]{:S(2)}) copy-start(bf16[56,1024]{1,0:T(8,128)(2,1)} %param.3) | copy-start | bytes 344068
  0.6 128.6 %copy-start = (bf16[56,1024]{1,0:T(8,128)(2,1)S(1)}, bf16[56,1024]{1,0:T(8,128)(2,1)}, u32[]{:S(2)}) copy-start(bf16[56,1024]{1,0:T(8,128)(2,1)} %param.4) | copy-start | bytes 344068
  1.7 9.2 %collective-permute-start = (bf16[2,56,1024]{2,1,0:T(8,128)(2,1)S(1)}, bf16[2,56,1024]{2,1,0:T(8,128)(2,1)S(1)}, u32[]{:S(2)}, u32[]{:S(2)}) collective-permute-start(bf16[2,56,1024]{2,1,0:T(8,128)(2,1)S(1)} %pad_maximum_fusion), channel_id=1, source_target_pairs={{0,2},{2,4},{4,6},{6,8},{8,10},{10,12},{12,14},{14,16},{16,18},{18... | collective-permute-start | bytes 688136 | tf_op jit(solution)/shard_map/ppermute | solution.py:27
  10.9 8.1 %collective-permute-start.1 = (bf16[2,56,1024]{2,1,0:T(8,128)(2,1)S(1)}, bf16[2,56,1024]{2,1,0:T(8,128)(2,1)S(1)}, u32[]{:S(2)}, u32[]{:S(2)}) collective-permute-start(bf16[2,56,1024]{2,1,0:T(8,128)(2,1)S(1)} %collective-permute-done), channel_id=1, source_target_pairs={{0,2},{2,4},{4,6},{6,8},{8,10},{10,12},{12,14},{14,16},{16,18},{18... | collective-permute-start | bytes 688136 | tf_op jit(solution)/shard_map/ppermute | solution.py:27
  19.0 8.1 %collective-permute-start.2 = (bf16[2,56,1024]{2,1,0:T(8,128)(2,1)S(1)}, bf16[2,56,1024]{2,1,0:T(8,128)(2,1)S(1)}, u32[]{:S(2)}, u32[]{:S(2)}) collective-permute-start(bf16[2,56,1024]{2,1,0:T(8,128)(2,1)S(1)} %collective-permute-done.1), channel_id=1, source_target_pairs={{0,2},{2,4},{4,6},{6,8},{8,10},{10,12},{12,14},{14,16},{16,18},{18... | collective-permute-start | bytes 688136 | tf_op jit(solution)/shard_map/ppermute | solution.py:27
  27.2 8.1 %collective-permute-start.3 = (bf16[2,56,1024]{2,1,0:T(8,128)(2,1)S(1)}, bf16[2,56,1024]{2,1,0:T(8,128)(2,1)S(1)}, u32[]{:S(2)}, u32[]{:S(2)}) collective-permute-start(bf16[2,56,1024]{2,1,0:T(8,128)(2,1)S(1)} %collective-permute-done.2), channel_id=1, source_target_pairs={{0,2},{2,4},{4,6},{6,8},{8,10},{10,12},{12,14},{14,16},{16,18},{18... | collective-permute-start | bytes 688136 | tf_op jit(solution)/shard_map/ppermute | solution.py:27
  35.3 8.1 %collective-permute-start.4 = (bf16[2,56,1024]{2,1,0:T(8,128)(2,1)S(1)}, bf16[2,56,1024]{2,1,0:T(8,128)(2,1)S(1)}, u32[]{:S(2)}, u32[]{:S(2)}) collective-permute-start(bf16[2,56,1024]{2,1,0:T(8,128)(2,1)S(1)} %collective-permute-done.3), channel_id=1, source_target_pairs={{0,2},{2,4},{4,6},{6,8},{8,10},{10,12},{12,14},{14,16},{16,18},{18... | collective-permute-start | bytes 688136 | tf_op jit(solution)/shard_map/ppermute | solution.py:27
  43.5 8.1 %collective-permute-start.5 = (bf16[2,56,1024]{2,1,0:T(8,128)(2,1)S(1)}, bf16[2,56,1024]{2,1,0:T(8,128)(2,1)S(1)}, u32[]{:S(2)}, u32[]{:S(2)}) collective-permute-start(bf16[2,56,1024]{2,1,0:T(8,128)(2,1)S(1)} %collective-permute-done.4), channel_id=1, source_target_pairs={{0,2},{2,4},{4,6},{6,8},{8,10},{10,12},{12,14},{14,16},{16,18},{18... | collective-permute-start | bytes 688136 | tf_op jit(solution)/shard_map/ppermute | solution.py:27
  51.6 8.1 %collective-permute-start.6 = (bf16[2,56,1024]{2,1,0:T(8,128)(2,1)S(1)}, bf16[2,56,1024]{2,1,0:T(8,128)(2,1)S(1)}, u32[]{:S(2)}, u32[]{:S(2)}) collective-permute-start(bf16[2,56,1024]{2,1,0:T(8,128)(2,1)S(1)} %collective-permute-done.5), channel_id=1, source_target_pairs={{0,2},{2,4},{4,6},{6,8},{8,10},{10,12},{12,14},{14,16},{16,18},{18... | collective-permute-start | bytes 688136 | tf_op jit(solution)/shard_map/ppermute | solution.py:27
  59.8 8.1 %collective-permute-start.7 = (bf16[2,56,1024]{2,1,0:T(8,128)(2,1)S(1)}, bf16[2,56,1024]{2,1,0:T(8,128)(2,1)S(1)}, u32[]{:S(2)}, u32[]{:S(2)}) collective-permute-start(bf16[2,56,1024]{2,1,0:T(8,128)(2,1)S(1)} %collective-permute-done.6), channel_id=1, source_target_pairs={{0,2},{2,4},{4,6},{6,8},{8,10},{10,12},{12,14},{14,16},{16,18},{18... | collective-permute-start | bytes 688136 | tf_op jit(solution)/shard_map/ppermute | solution.py:27
  67.9 8.1 %collective-permute-start.8 = (bf16[2,56,1024]{2,1,0:T(8,128)(2,1)S(1)}, bf16[2,56,1024]{2,1,0:T(8,128)(2,1)S(1)}, u32[]{:S(2)}, u32[]{:S(2)}) collective-permute-start(bf16[2,56,1024]{2,1,0:T(8,128)(2,1)S(1)} %collective-permute-done.7), channel_id=1, source_target_pairs={{0,2},{2,4},{4,6},{6,8},{8,10},{10,12},{12,14},{14,16},{16,18},{18... | collective-permute-start | bytes 688136 | tf_op jit(solution)/shard_map/ppermute | solution.py:27
  76.1 8.1 %collective-permute-start.9 = (bf16[2,56,1024]{2,1,0:T(8,128)(2,1)S(1)}, bf16[2,56,1024]{2,1,0:T(8,128)(2,1)S(1)}, u32[]{:S(2)}, u32[]{:S(2)}) collective-permute-start(bf16[2,56,1024]{2,1,0:T(8,128)(2,1)S(1)} %collective-permute-done.8), channel_id=1, source_target_pairs={{0,2},{2,4},{4,6},{6,8},{8,10},{10,12},{12,14},{14,16},{16,18},{18... | collective-permute-start | bytes 688136 | tf_op jit(solution)/shard_map/ppermute | solution.py:27
  84.2 8.1 %collective-permute-start.10 = (bf16[2,56,1024]{2,1,0:T(8,128)(2,1)S(1)}, bf16[2,56,1024]{2,1,0:T(8,128)(2,1)S(1)}, u32[]{:S(2)}, u32[]{:S(2)}) collective-permute-start(bf16[2,56,1024]{2,1,0:T(8,128)(2,1)S(1)} %collective-permute-done.9), channel_id=1, source_target_pairs={{0,2},{2,4},{4,6},{6,8},{8,10},{10,12},{12,14},{14,16},{16,18},{18... | collective-permute-start | bytes 688136 | tf_op jit(solution)/shard_map/ppermute | solution.py:27
  92.3 8.1 %collective-permute-start.11 = (bf16[2,56,1024]{2,1,0:T(8,128)(2,1)S(1)}, bf16[2,56,1024]{2,1,0:T(8,128)(2,1)S(1)}, u32[]{:S(2)}, u32[]{:S(2)}) collective-permute-start(bf16[2,56,1024]{2,1,0:T(8,128)(2,1)S(1)} %collective-permute-done.10), channel_id=1, source_target_pairs={{0,2},{2,4},{4,6},{6,8},{8,10},{10,12},{12,14},{14,16},{16,18},{18... | collective-permute-start | bytes 688136 | tf_op jit(solution)/shard_map/ppermute | solution.py:27
  100.5 8.1 %collective-permute-start.12 = (bf16[2,56,1024]{2,1,0:T(8,128)(2,1)S(1)}, bf16[2,56,1024]{2,1,0:T(8,128)(2,1)S(1)}, u32[]{:S(2)}, u32[]{:S(2)}) collective-permute-start(bf16[2,56,1024]{2,1,0:T(8,128)(2,1)S(1)} %collective-permute-done.11), channel_id=1, source_target_pairs={{0,2},{2,4},{4,6},{6,8},{8,10},{10,12},{12,14},{14,16},{16,18},{18... | collective-permute-start | bytes 688136 | tf_op jit(solution)/shard_map/ppermute | solution.py:27
  108.6 0.7 copy-start.2
  109.3 8.2 %collective-permute-start.13 = (bf16[2,56,1024]{2,1,0:T(8,128)(2,1)S(1)}, bf16[2,56,1024]{2,1,0:T(8,128)(2,1)}, u32[]{:S(2)}, u32[]{:S(2)}) collective-permute-start(bf16[2,56,1024]{2,1,0:T(8,128)(2,1)S(1)} %collective-permute-done.12), channel_id=1, source_target_pairs={{0,2},{2,4},{4,6},{6,8},{8,10},{10,12},{12,14},{14,16},{16,18},{18... | collective-permute-start | bytes 688136 | tf_op jit(solution)/shard_map/ppermute | solution.py:27
  117.5 8.5 %collective-permute-start.14 = (bf16[2,56,1024]{2,1,0:T(8,128)(2,1)}, bf16[2,56,1024]{2,1,0:T(8,128)(2,1)}, u32[]{:S(2)}, u32[]{:S(2)}) collective-permute-start(bf16[2,56,1024]{2,1,0:T(8,128)(2,1)} %collective-permute-done.13), channel_id=1, source_target_pairs={{0,2},{2,4},{4,6},{6,8},{8,10},{10,12},{12,14},{14,16},{16,18},{18... | collective-permute-start | bytes 688136 | tf_op jit(solution)/shard_map/ppermute | solution.py:27
  121.3 9.8 %copy-start.3 = (bf16[2,56,1024]{2,1,0:T(8,128)(2,1)S(1)}, bf16[2,56,1024]{2,1,0:T(8,128)(2,1)}, u32[]{:S(2)}) copy-start(bf16[2,56,1024]{2,1,0:T(8,128)(2,1)} %copy-done.2) | copy-start | bytes 688132
